TPU v7x, 32 devices: a whole 2x2x4 slice. The times are simulated.
32 devices in a mesh: site: 2 (over y), pts: 16 (over z, x, core).
Axes of the slice: x: 2, y: 2, z: 4, core: 2. Of those that a mesh axis runs over, the one named last changes fastest.
Arguments:
- green_tensors: bfloat16 [512, 4, 6, 2, 1024], P(('site', 'pts')), parts along dimension 0, may hold values from -6 to 6
- block_lists: int32 [32, 32], P(('site', 'pts')), parts along dimension 0, may hold values from 0 to 255, as said below
- block_count: int32 [32], P(('site', 'pts')), parts along dimension 0, may hold values from 1 to 32
- onset_steps: int32 [32, 16, 128], P(('site', 'pts')), parts along dimension 0, may hold values from 0 to 255
- slip_amount: float32 [32, 16, 128], P(('site', 'pts')), parts along dimension 0, may hold values from 0.2 to 2
- mechanism: float32 [32, 6], P(('site', 'pts')), parts along dimension 0, may hold values from -2.4 to 2.4
- slip_rate: float32 [32, 16, 128], P(('site', 'pts')), parts along dimension 0, may hold values from 0.005 to 0.05
Outputs:
- seismograms: float32 [32, 16, 2, 1024], P(('site', 'pts')), parts along dimension 0
There are 2 independent parts, one for each index of `site`. A program takes and returns all parts, laid end to end along the dimension named above; each array names one. Nothing has to cross between parts.
Inputs may be any that keep to these rules, and one draw needn't show every extreme that they name: `block_lists`: numbers of point blocks; the ruptures held by one device name at most 2 entries in blocks held by any one device, and exactly 2 for some holder.
All inputs are finite; a program needn't handle non-finite values.
Results may differ from a plain program's by a relative error of at most 0.0003.
Values may be sent and summed in bfloat16 or wider, within the bound.
No kernel may reach another device: no remote copies, remote signals or barrier semaphores. Data moves between devices by JAX's collectives and lax.ppermute only.
A program may use at most 128 MiB of HBM per device.

v0:
```python
import jax
import jax.numpy as jnp
from jax import lax
from jax.sharding import PartitionSpec as P

MAXON = 256


def lag_traces(traces, onsets):
    length = traces.shape[-1]
    shifted_all = traces
    for bit_index in range((MAXON - 1).bit_length()):
        stride = 1 << bit_index
        shifted = jnp.pad(shifted_all, ((0, 0), (0, 0), (stride, 0)))[:, :, :length]
        bit_set = jnp.bitwise_and(jnp.right_shift(onsets, bit_index), 1) == 1
        shifted_all = jnp.where(bit_set[:, None, None], shifted, shifted_all)
    return shifted_all


def weighted_sum(traces, weights, onsets):

    def per_variation(weight_row, onset_row):
        return jnp.sum(weight_row[:, None, None] * lag_traces(traces, onset_row), axis=0)

    return jax.vmap(per_variation)(weights, onsets)


def convolve_rate(motion, slip_rate):
    taps = slip_rate.shape[-1]
    length = motion.shape[-1]
    offset = jnp.arange(taps, dtype=jnp.int32)[None, :] - jnp.arange(taps, dtype=jnp.int32)[:, None]
    near = jnp.where(offset >= 0, jnp.take(slip_rate, jnp.clip(offset, 0, taps - 1), axis=-1), 0.0)
    far = jnp.where(
        offset < 0, jnp.take(slip_rate, jnp.clip(offset + taps, 0, taps - 1), axis=-1), 0.0
    )
    blocked = motion.reshape(motion.shape[:-1] + (length // taps, taps))
    earlier = jnp.pad(blocked, ((0, 0), (0, 0), (0, 0), (1, 0), (0, 0)))[:, :, :, :-1, :]
    result = jnp.einsum("rvcbi,rvij->rvcbj", blocked, near, precision=lax.Precision.HIGHEST)
    result = result + jnp.einsum("rvcbi,rvij->rvcbj", earlier, far, precision=lax.Precision.HIGHEST)
    return result.reshape(motion.shape)


def local(green_tensors, block_lists, block_count, onset_steps, slip_amount, mechanism, slip_rate):
    held = green_tensors.shape[0]
    points = green_tensors.shape[1]
    length = green_tensors.shape[-1]
    ruptures, listed = block_lists.shape
    devices = lax.axis_size("pts")
    capacity = max(1, ruptures * listed // devices)
    own_index = lax.axis_index("pts")
    entries = ruptures * listed
    every_list = lax.all_gather(block_lists, "pts", axis=0, tiled=True)
    holder = every_list // held
    local_block = every_list % held
    order = jnp.arange(entries, dtype=jnp.int32)
    earlier_same = (holder[:, :, None] == holder[:, None, :]) & (
        order[None, None, :] < order[None, :, None]
    )
    slot_rank = jnp.sum(earlier_same.astype(jnp.int32), axis=2)
    slot_ids = jnp.arange(capacity, dtype=jnp.int32)
    chosen = (
        (holder == own_index)[:, None, :] & (slot_rank[:, None, :] == slot_ids[None, :, None])
    ).astype(jnp.int32)
    slot_block = jnp.sum(chosen * local_block[:, None, :], axis=2)
    my_holder = block_lists.reshape(entries) // held
    my_rank = lax.dynamic_index_in_dim(slot_rank, own_index, 0, keepdims=False)
    source_row = my_holder * capacity + my_rank
    kept_mask = (jnp.arange(listed, dtype=jnp.int32)[None, :] < block_count[:, None]).astype(
        jnp.float32
    )
    weights = slip_amount * jnp.repeat(kept_mask, points, axis=1)[:, None, :]

    def rupture_motion(inputs):
        rupture_traces, weight_rows, onset_rows = inputs
        return weighted_sum(rupture_traces.reshape(-1, 2, length), weight_rows, onset_rows)

    outgoing = jnp.take(green_tensors, slot_block.reshape(-1), axis=0)
    outgoing = outgoing.reshape((devices, capacity) + green_tensors.shape[1:])
    incoming = lax.all_to_all(outgoing, "pts", split_axis=0, concat_axis=0, tiled=True)
    flat_rows = incoming.reshape((devices * capacity,) + green_tensors.shape[1:])
    needed = jnp.take(flat_rows, source_row, axis=0)
    traces = jnp.einsum(
        "rkpsct,rs->rkpct",
        needed.reshape((ruptures, listed) + green_tensors.shape[1:]).astype(jnp.float32),
        mechanism,
        precision=lax.Precision.HIGHEST,
    )
    motion = lax.map(rupture_motion, (traces, weights, onset_steps))
    return convolve_rate(motion, slip_rate)


def solution(mesh):
    in_specs = (
        P(("site", "pts"), None, None, None, None),
        P(("site", "pts"), None),
        P(("site", "pts")),
        P(("site", "pts"), None, None),
        P(("site", "pts"), None, None),
        P(("site", "pts"), None),
        P(("site", "pts"), None, None),
    )
    out_specs = P(("site", "pts"), None, None, None)
    return jax.shard_map(local, mesh=mesh, in_specs=in_specs, out_specs=out_specs, check_vma=False)
```

profile of v0, /device:TPU:0, one launch (start us, length us, event | category | flops | bytes accessed | tf_op | source)
XLA Modules:
  0.0 280.7 jit_solution(6019575131359495665)
XLA Ops:
  0.0 23.4 %all-gather = s32[16,1,32]{2,1,0:T(1,128)S(1)} all-gather(s32[1,1,32]{2,1,0:T(1,128)} %bitcast.123), channel_id=1, replica_groups=mesh['site'=2,'pts'=16] {'pts'}, dimensions={0}, use_global_device_ids=true | all-gather | bytes 2176 | tf_op jit(solution)/shard_map/all_gather | solution.py:52
  23.4 0.5 convert_reduce_fusion
  23.9 0.1 select_reduce_fusion
  24.1 0.1 reshape.339
  24.2 0.1 copy.20
  24.3 8.4 %gather_fusion = bf16[32,4,6,2,1024]{4,3,2,1,0:T(2,128)(2,1)} fusion(bf16[16,4,6,2,1024]{4,3,2,1,0:T(2,128)(2,1)S(1)} %copy-done, s32[1024]{0:T(1024)S(1)} %pad_clamp_fusion.1), kind=kCustom, calls=%fused_computation.2 | custom fusion | bytes 6291584 | tf_op jit(solution)/shard_map/jit(_take)/gather | solution.py:77
  32.7 6.5 %broadcast_select_fusion.2 = bf16[16,2,4,6,2,1024]{5,4,3,2,1,0:T(2,128)(2,1)} fusion(bf16[16,2,4,6,2,1024]{5,4,3,2,1,0:T(2,128)(2,1)} %bitcast.116, pred[16,2]{1,0:T(8,128)(4,1)S(1)} %copy.20), kind=kLoop, calls=%fused_computation.22 | loop fusion | flops 1572864 | bytes 6291488 | tf_op jit(solution)/shard_map/jit(_take)/select_n | solution.py:77
  39.2 4.7 %all-to-all-start = ((bf16[16,2,4,6,2,1024]{5,4,3,2,1,0:T(2,128)(2,1)}), bf16[16,2,4,6,2,1024]{5,4,3,2,1,0:T(2,128)(2,1)}, u32[]{:S(2)}, u32[]{:S(2)}) async-start(bf16[16,2,4,6,2,1024]{5,4,3,2,1,0:T(2,128)(2,1)} %broadcast_select_fusion.2), calls=%async_computation | async-start | bytes 6291456 | tf_op jit(solution)/shard_map/all_to_all | solution.py:79
  44.6 0.1 broadcast_in_dim.161
  44.7 0.1 copy.22
  44.9 54.8 %gather_fusion.2 = f32[16384,16]{1,0:T(8,128)} fusion(f32[16,128]{0,1:T(8,128)S(1)} %bitcast.113, s32[16384]{0:T(1024)S(1)} %bitcast_clamp_fusion.1), kind=kCustom, calls=%fused_computation.clone | custom fusion | bytes 2162688 | tf_op jit(solution)/shard_map/jit(_take)/gather | solution.py:32
  99.6 5.2 %copy.23 = f32[128,128,16]{1,0,2:T(8,128)S(1)} copy(f32[128,128,16]{2,1,0:T(8,128)} %bitcast.118) | data formatting | bytes 2097152 | tf_op jit(solution)/shard_map/jit(_take)/gather | solution.py:32
  104.9 54.8 %gather_fusion.3 = f32[16384,16]{1,0:T(8,128)} fusion(f32[16,128]{0,1:T(8,128)S(1)} %bitcast.114, s32[16384]{0:T(1024)S(1)} %bitcast_clamp_fusion), kind=kCustom, calls=%fused_computation.1.clone | custom fusion | bytes 2162688 | tf_op jit(solution)/shard_map/jit(_take)/gather | solution.py:34
  159.7 6.1 %copy.25 = f32[128,128,16]{1,0,2:T(8,128)} copy(f32[128,128,16]{2,1,0:T(8,128)} %bitcast.117) | data formatting | bytes 2097152 | tf_op jit(solution)/shard_map/jit(_take)/gather | solution.py:34
  166.0 10.3 %gather_fusion.1 = bf16[32,4,6,2,1024]{4,3,2,1,0:T(2,128)(2,1)} fusion(bf16[32,4,6,2,1024]{4,3,2,1,0:T(2,128)(2,1)} %bitcast.16, s32[1024]{0:T(1024)S(1)} %pad_clamp_fusion), kind=kCustom, calls=%fused_computation.3 | custom fusion | bytes 6291584 | tf_op jit(solution)/shard_map/jit(_take)/gather | solution.py:81
  176.3 4.7 %broadcast_select_fusion.1 = bf16[32,4,6,2,1024]{4,3,2,1,0:T(2,128)(2,1)S(1)} fusion(bf16[32,4,6,2,1024]{4,3,2,1,0:T(2,128)(2,1)} %gather_fusion.1, pred[32]{0:T(512)(128)(4,1)S(1)} %compare_and_fusion.1), kind=kLoop, calls=%fused_computation.21 | loop fusion | flops 1572864 | bytes 6291488 | tf_op jit(solution)/shard_map/jit(_take)/select_n | solution.py:81
  181.0 3.6 %fusion.9 = f32[1,128,2,1024]{3,0,2,1:T(1,128)S(1)} fusion(bf16[128,2,1024,6]{2,1,3,0:T(2,128)(2,1)S(1)} %bitcast.115, f32[1,6]{1,0:T(1,128)S(1)} %copy-done.6), kind=kOutput, calls=%fused_computation.23 | convolution fusion | flops 18874368 | bytes 4194328 | tf_op jit(solution)/shard_map/rkpsct,rs->rkpct/dot_general | solution.py:82
  184.6 0.3 copy.34
  184.9 0.3 pad_slice_fusion.7
  185.3 6.9 %broadcast_select_fusion = f32[16,128,2,1024]{3,1,2,0:T(8,128)} fusion(f32[128,2,1024]{2,0,1:T(8,128)S(1)} %bitcast.120, f32[128,2,1024]{2,0,1:T(8,128)S(1)} %pad_slice_fusion.7, pred[16,128]{1,0:T(8,128)(4,1)S(1)} %get-tuple-element.29), kind=kLoop, calls=%fused_computation.20 | loop fusion | flops 4194304 | bytes 18876416 | tf_op jit(solution)/shard_map/while/body/eval_jaxpr/vmap(jit(_where))/select_n | solution.py:16
  192.2 14.9 %fusion = f32[16,128,2,1024]{3,1,2,0:T(8,128)S(1)} fusion(f32[16,128,2,1024]{3,1,2,0:T(8,128)} %broadcast_select_fusion, pred[16,128]{1,0:T(8,128)(4,1)S(1)} %get-tuple-element.30), kind=kLoop, calls=%fused_computation.11 | loop fusion | flops 4194304 | bytes 33556480 | tf_op jit(solution)/shard_map/while/body/eval_jaxpr/vmap(jit(_where))/select_n | solution.py:16
  207.1 8.4 %fusion.1 = f32[16,128,2,1024]{3,1,2,0:T(8,128)} fusion(f32[16,128,2,1024]{3,1,2,0:T(8,128)S(1)} %fusion, pred[16,128]{1,0:T(8,128)(4,1)S(1)} %get-tuple-element.24), kind=kLoop, calls=%fused_computation.12 | loop fusion | flops 4194304 | bytes 33556480 | tf_op jit(solution)/shard_map/while/body/eval_jaxpr/vmap(jit(_where))/select_n | solution.py:16
  215.4 14.9 %fusion.2 = f32[16,128,2,1024]{3,1,2,0:T(8,128)S(1)} fusion(f32[16,128,2,1024]{3,1,2,0:T(8,128)} %fusion.1, pred[16,128]{1,0:T(8,128)(4,1)S(1)} %get-tuple-element.25), kind=kLoop, calls=%fused_computation.13 | loop fusion | flops 4194304 | bytes 33556480 | tf_op jit(solution)/shard_map/while/body/eval_jaxpr/vmap(jit(_where))/select_n | solution.py:16
  230.3 8.4 %fusion.3 = f32[16,128,2,1024]{3,1,2,0:T(8,128)} fusion(f32[16,128,2,1024]{3,1,2,0:T(8,128)S(1)} %fusion.2, pred[16,128]{1,0:T(8,128)(4,1)S(1)} %get-tuple-element.26), kind=kLoop, calls=%fused_computation.14 | loop fusion | flops 4194304 | bytes 33556480 | tf_op jit(solution)/shard_map/while/body/eval_jaxpr/vmap(jit(_where))/select_n | solution.py:16
  238.7 19.1 %fusion.4 = f32[16,128,2,1024]{3,1,2,0:T(8,128)} fusion(f32[16,128,2,1024]{3,1,2,0:T(8,128)} %fusion.3, pred[16,128]{1,0:T(8,128)(4,1)S(1)} %get-tuple-element.27), kind=kLoop, calls=%fused_computation.15 | loop fusion | flops 4194304 | bytes 33556480 | tf_op jit(solution)/shard_map/while/body/eval_jaxpr/vmap(jit(_where))/select_n | solution.py:16
  257.8 14.9 %fusion.5 = f32[16,128,2,1024]{3,1,2,0:T(8,128)S(1)} fusion(f32[16,128,2,1024]{3,1,2,0:T(8,128)} %fusion.4, pred[16,128]{1,0:T(8,128)(4,1)S(1)} %get-tuple-element.28), kind=kLoop, calls=%fused_computation.16 | loop fusion | flops 4194304 | bytes 33556480 | tf_op jit(solution)/shard_map/while/body/eval_jaxpr/vmap(jit(_where))/select_n | solution.py:16
  272.7 3.7 %fusion.8 = f32[16,2,1024]{2,1,0:T(2,128)S(1)} fusion(f32[16,128,2,1024]{3,1,2,0:T(8,128)S(1)} %fusion.5, f32[16,128]{1,0:T(8,128)S(1)} %multiply_bitcast_fusion, pred[16,128]{1,0:T(8,128)(4,1)S(1)} %get-tuple-element.22), kind=kLoop, calls=%fused_computation.19 | loop fusion | flops 12550144 | bytes 16918528 | tf_op jit(solution)/shard_map/while/body/eval_jaxpr/vmap()/reduce_sum | solution.py:23
  276.4 0.1 reshape.343
  276.5 0.1 reshape.345
  276.6 1.0 fusion.14
  277.7 2.3 convolution_add_fusion
  279.9 0.7 reshape.348
  (33 shorter events, 0.5 us)
Async XLA Ops:
  0.0 24.3 %copy-start = (bf16[16,4,6,2,1024]{4,3,2,1,0:T(2,128)(2,1)S(1)}, bf16[16,4,6,2,1024]{4,3,2,1,0:T(2,128)(2,1)}, u32[]{:S(2)}) copy-start(bf16[16,4,6,2,1024]{4,3,2,1,0:T(2,128)(2,1)} %param.9) | copy-start | bytes 4718596
  24.3 20.4 %copy-start.2 = (f32[1,16,128]{2,1,0:T(8,128)S(1)}, f32[1,16,128]{2,1,0:T(8,128)}, u32[]{:S(2)}) copy-start(f32[1,16,128]{2,1,0:T(8,128)} %param.15) | copy-start | bytes 24580
  39.2 126.8 %all-to-all-start = ((bf16[16,2,4,6,2,1024]{5,4,3,2,1,0:T(2,128)(2,1)}), bf16[16,2,4,6,2,1024]{5,4,3,2,1,0:T(2,128)(2,1)}, u32[]{:S(2)}, u32[]{:S(2)}) async-start(bf16[16,2,4,6,2,1024]{5,4,3,2,1,0:T(2,128)(2,1)} %broadcast_select_fusion.2), calls=%async_computation | async-start | bytes 6291456 | tf_op jit(solution)/shard_map/all_to_all | solution.py:79
  104.9 60.9 %copy-start.5 = (s32[1,32]{1,0:T(1,128)S(1)}, s32[1,32]{1,0:T(1,128)}, u32[]{:S(2)}) copy-start(s32[1,32]{1,0:T(1,128)} %param.10) | copy-start | bytes 388
  104.9 61.0 %copy-start.4 = (f32[1,16,128]{2,1,0:T(8,128)S(1)}, f32[1,16,128]{2,1,0:T(8,128)}, u32[]{:S(2)}) copy-start(f32[1,16,128]{2,1,0:T(8,128)} %param.13) | copy-start | bytes 24580
  104.9 61.0 %copy-start.3 = (s32[1,16,128]{2,1,0:T(8,128)S(1)}, s32[1,16,128]{2,1,0:T(8,128)}, u32[]{:S(2)}) copy-start(s32[1,16,128]{2,1,0:T(8,128)} %param.12) | copy-start | bytes 24580
  165.7 15.2 %copy-start.6 = (f32[1,6]{1,0:T(1,128)S(1)}, f32[1,6]{1,0:T(1,128)}, u32[]{:S(2)}) copy-start(f32[1,6]{1,0:T(1,128)} %param.14) | copy-start | bytes 76
  272.7 8.0 %copy-start.1 = (bf16[16,4,6,2,1024]{4,3,2,1,0:T(2,128)(2,1)S(1)}, bf16[16,4,6,2,1024]{4,3,2,1,0:T(2,128)(2,1)}, u32[]{:S(2)}) copy-start(bf16[16,4,6,2,1024]{4,3,2,1,0:T(2,128)(2,1)} %param.9) | copy-start | bytes 4718596
where the time goes:
time: 281 us
  local copies, waits for them, and re-layouts  142 us (51%)
  other arithmetic  103 us (37%)
  blocking collectives  23.4 us (8%)
  matrix products  6.9 us (2%)
  starting transfers between devices  4.69 us (2%)
    select_n x7, other arithmetic, lag_traces(): shifted_all = jnp.where(bit_set[:, None, None], shifted, shifted_all)  87.4 us
    gather x2, local copies, waits for them, and re-layouts, convolve_rate(): jnp.take(slip_rate, jnp.clip(offset + taps, 0, taps - 1), axis=-1)  60.8 us
    gather x2, local copies, waits for them, and re-layouts, convolve_rate(): jnp.take(slip_rate, jnp.clip(offset, 0, taps - 1), axis=-1)  60 us
    all_gather x1, blocking collectives, local(): every_list = lax.all_gather(block_lists, 'pts', axis=0, tiled=True)  23.4 us
    gather x1, local copies, waits for them, and re-layouts, local(): needed = jnp.take(flat_rows, source_row, axis=0)  10.3 us
    gather x1, local copies, waits for them, and re-layouts, local(): outgoing = jnp.take(green_tensors, slot_block.reshape(-1), axis=0)  8.38 us
    select_n x2, other arithmetic, local(): outgoing = jnp.take(green_tensors, slot_block.reshape(-1), axis=0)  6.45 us
  transfers between devices with their start and end apart: 1, of which 0 were waited for; matrix products, arithmetic and copies ran while one was open for 43% of the time, Pallas kernels for 0%

commit v1 on v0

v1 whole, which is shorter than its diff:
```python
import functools

import jax
import jax.numpy as jnp
from jax import lax
from jax.experimental import pallas as pl
from jax.experimental.pallas import tpu as pltpu
from jax.sharding import PartitionSpec as P

MAXON = 256
FINE = 8
LANES = 128
F32 = jnp.float32
BF16 = jnp.bfloat16


def split(x):
    hi = x.astype(BF16)
    return hi, (x - hi.astype(F32)).astype(BF16)


def dot3(a_hi, a_lo, b_hi, b_lo):
    dot = functools.partial(jnp.dot, preferred_element_type=F32)
    return dot(a_hi, b_hi) + (dot(a_hi, b_lo) + dot(a_lo, b_hi))


def contract_kernel(block_ref, mech_ref, tensors_ref, out_ref, *, slots, points, strains):
    def one_slot(i, carry):
        block = block_ref[i]
        source = i // slots
        factors = [mech_ref[source, s] for s in range(strains)]
        for p in range(points):
            total = factors[0] * tensors_ref[block, p, 0].astype(F32)
            for s in range(1, strains):
                total = total + factors[s] * tensors_ref[block, p, s].astype(F32)
            out_ref[i, p] = total
        return carry

    lax.fori_loop(0, out_ref.shape[0], one_slot, 0, unroll=2)


def prepare_kernel(onset_ref, weight_ref, rate_ref, a_hi_ref, a_lo_ref, t_hi_ref, t_lo_ref):
    variations, points = onset_ref.shape
    taps = rate_ref.shape[1]
    onsets = onset_ref[...]
    weights = weight_ref[...]
    w_hi = weights.astype(BF16).astype(F32)
    w_lo = weights - w_hi
    for coarse in range(MAXON // FINE):
        for fine in range(FINE):
            hit = onsets == coarse * FINE + fine
            rows = pl.ds(coarse * variations, variations)
            cols = pl.ds(fine * points, points)
            a_hi_ref[rows, cols] = jnp.where(hit, w_hi, 0.0).astype(BF16)
            a_lo_ref[rows, cols] = jnp.where(hit, w_lo, 0.0).astype(BF16)
    row = lax.broadcasted_iota(jnp.int32, (taps, taps), 0)
    col = lax.broadcasted_iota(jnp.int32, (taps, taps), 1)
    for v in range(variations):
        rates = jnp.broadcast_to(rate_ref[pl.ds(v, 1), :], (taps, taps))
        turned = pltpu.roll(rates, 0, 1, stride=1, stride_axis=0)
        hi, lo = split(jnp.where(col >= row, turned, 0.0))
        t_hi_ref[v, pl.ds(0, taps), :] = hi
        t_lo_ref[v, pl.ds(0, taps), :] = lo
        hi, lo = split(jnp.where(col < row, turned, 0.0))
        t_hi_ref[v, pl.ds(taps, taps), :] = hi
        t_lo_ref[v, pl.ds(taps, taps), :] = lo


def synth_kernel(row_ref, got_ref, a_hi_ref, a_lo_ref, t_hi_ref, t_lo_ref, out_ref,
                 base_ref, x_hi_ref, x_lo_ref, acc_ref, motion_ref, *, listed, points):
    variations, rows = out_ref.shape[:2]
    q = listed * points
    comps = 2
    blocks = rows // comps

    def place(k, carry):
        source = row_ref[k]
        for p in range(points):
            base_ref[pl.ds(pl.multiple_of((k * points + p) * rows, rows), rows), :] = got_ref[source, p]
        return carry

    lax.fori_loop(0, listed, place, 0, unroll=4)
    lane = lax.broadcasted_iota(jnp.int32, (q, LANES), 1)
    for c in range(comps):
        before = [jnp.zeros((q, LANES), F32)] * FINE
        for block in range(blocks):
            r = block * comps + c
            here = base_ref[pl.ds(r, q, stride=rows), :]
            at = pl.ds((c * blocks + block) * LANES, LANES)
            for fine in range(FINE):
                turned = pltpu.roll(here, fine, 1) if fine else here
                value = jnp.where(lane >= fine, turned, before[fine]) if fine else here
                hi, lo = split(value)
                x_hi_ref[pl.ds(fine * q, q), at] = hi
                x_lo_ref[pl.ds(fine * q, q), at] = lo
                before[fine] = turned
    acc_ref[...] = dot3(a_hi_ref[...], a_lo_ref[...], x_hi_ref[...], x_lo_ref[...])
    lane = lax.broadcasted_iota(jnp.int32, (variations, LANES), 1)
    zero = jnp.zeros((variations, LANES), F32)
    half = LANES // FINE
    far_count = MAXON // LANES
    pad = motion_ref.shape[0] // variations
    motion_ref[...] = jnp.zeros(motion_ref.shape, F32)
    for c in range(comps):
        before = [zero] * half
        for block in range(blocks):
            total = zero
            for coarse in range(half):
                value = zero
                for far in range(far_count):
                    if block - far < 0:
                        continue
                    at = pl.ds((c * blocks + block - far) * LANES, LANES)
                    value = value + acc_ref[pl.ds((far * half + coarse) * variations, variations), at]
                turned = pltpu.roll(value, coarse * FINE, 1) if coarse else value
                total = total + (jnp.where(lane >= coarse * FINE, turned, before[coarse]) if coarse else turned)
                before[coarse] = turned
            motion_ref[pl.ds(FINE + block * comps + c, variations, stride=pad), :] = total
    for v in range(variations):
        here = motion_ref[pl.ds(v * pad + FINE, rows), :]
        earlier = motion_ref[pl.ds(v * pad + FINE - comps, rows), :]
        h_hi, h_lo = split(jnp.concatenate([here, earlier], axis=1))
        out_ref[v] = dot3(h_hi, h_lo, t_hi_ref[v], t_lo_ref[v])


VMEM = pl.BlockSpec(memory_space=pltpu.VMEM)
SMEM = pl.BlockSpec(memory_space=pltpu.SMEM)


def local(green_tensors, block_lists, block_count, onset_steps, slip_amount, mechanism, slip_rate):
    held, points, strains, comps, length = green_tensors.shape
    ruptures, listed = block_lists.shape
    variations = onset_steps.shape[1]
    taps = slip_rate.shape[-1]
    devices = lax.axis_size("pts")
    capacity = max(1, ruptures * listed // devices)
    blocks = length // LANES
    rows = blocks * comps
    q = listed * points

    tensors = green_tensors.reshape(held, points, strains, comps, blocks, LANES)
    tensors = tensors.transpose(0, 1, 2, 4, 3, 5).reshape(held, points, strains, rows, LANES)

    entries = block_lists.reshape(ruptures * listed)
    holder = entries // held
    order = jnp.arange(ruptures * listed, dtype=jnp.int32)
    same = (holder[:, None] == holder[None, :]) & (order[None, :] < order[:, None])
    rank = jnp.sum(same.astype(jnp.int32), axis=1)
    slot_of = holder * capacity + rank
    slot_ids = jnp.arange(devices * capacity, dtype=jnp.int32)
    wanted = jnp.sum(
        jnp.where(slot_of[None, :] == slot_ids[:, None], (entries % held)[None, :], 0), axis=1
    )
    request = jnp.concatenate(
        [
            wanted.astype(F32).reshape(devices, capacity),
            jnp.broadcast_to(mechanism.reshape(1, strains), (devices, strains)),
        ],
        axis=1,
    )
    asked = lax.all_to_all(request, "pts", split_axis=0, concat_axis=0, tiled=True)
    block_of = asked[:, :capacity].astype(jnp.int32).reshape(devices * capacity)
    factors = asked[:, capacity:]

    kept = (jnp.arange(q, dtype=jnp.int32) // points) < block_count[0]
    weights = jnp.where(kept[None, :], slip_amount[0], 0.0)
    coarse_rows = MAXON // FINE * variations
    prepared = pl.pallas_call(
        prepare_kernel,
        name="prepare",
        out_shape=(
            jax.ShapeDtypeStruct((coarse_rows, FINE * q), BF16),
            jax.ShapeDtypeStruct((coarse_rows, FINE * q), BF16),
            jax.ShapeDtypeStruct((variations, 2 * taps, taps), BF16),
            jax.ShapeDtypeStruct((variations, 2 * taps, taps), BF16),
        ),
        in_specs=[VMEM, VMEM, VMEM],
        out_specs=(VMEM, VMEM, VMEM, VMEM),
    )(onset_steps[0], weights, slip_rate[0])

    outgoing = pl.pallas_call(
        functools.partial(contract_kernel, slots=capacity, points=points, strains=strains),
        name="contract",
        out_shape=jax.ShapeDtypeStruct((devices * capacity, points, rows, LANES), F32),
        in_specs=[SMEM, SMEM, VMEM],
        out_specs=VMEM,
    )(block_of, factors, tensors)
    incoming = lax.all_to_all(outgoing, "pts", split_axis=0, concat_axis=0, tiled=True)

    result = pl.pallas_call(
        functools.partial(synth_kernel, listed=listed, points=points),
        name="synthesize",
        out_shape=jax.ShapeDtypeStruct((variations, rows, LANES), F32),
        in_specs=[SMEM, VMEM, VMEM, VMEM, VMEM, VMEM],
        out_specs=VMEM,
        scratch_shapes=[
            pltpu.VMEM((q * rows, LANES), F32),
            pltpu.VMEM((FINE * q, rows * LANES), BF16),
            pltpu.VMEM((FINE * q, rows * LANES), BF16),
            pltpu.VMEM((coarse_rows, rows * LANES), F32),
            pltpu.VMEM((variations * (rows + FINE), LANES), F32),
        ],
    )(slot_of, incoming, *prepared)
    result = result.reshape(variations, blocks, comps, LANES).transpose(0, 2, 1, 3)
    return result.reshape(1, variations, comps, length)


def solution(mesh):
    in_specs = (
        P(("site", "pts"), None, None, None, None),
        P(("site", "pts"), None),
        P(("site", "pts")),
        P(("site", "pts"), None, None),
        P(("site", "pts"), None, None),
        P(("site", "pts"), None),
        P(("site", "pts"), None, None),
    )
    out_specs = P(("site", "pts"), None, None, None)
    return jax.shard_map(local, mesh=mesh, in_specs=in_specs, out_specs=out_specs, check_vma=False)
```

time: 281 us -> 61.2 us (0.22)
  the two profiles are of different devices: /device:TPU:0 before, /device:TPU:13 now
where the time goes in v1:
time: 61.2 us; the launch traced here: 60.9 us
  waiting for transfers between devices  19.7 us (32%)
  Pallas kernels  17.7 us (29%)
  blocking collectives  11.1 us (18%)
  starting transfers between devices  5.38 us (9%)
  local copies, waits for them, and re-layouts  3.42 us (6%)
  other arithmetic  2.92 us (5%)
  between operations  0.69 us (1%)
    all_to_all x1, waiting for transfers between devices, local(): lax.all_to_all(outgoing, 'pts', split_axis=0, concat_axis=0, tiled=True)  19.7 us
    pallas_call x1, Pallas kernels, local(): pl.pallas_call(functools.partial(synth_kernel, listed=listed, points=poin...  11.1 us
    all_to_all x1, blocking collectives, local(): lax.all_to_all(request, 'pts', split_axis=0, concat_axis=0, tiled=True)  11.1 us
    all_to_all x1, starting transfers between devices, local(): lax.all_to_all(outgoing, 'pts', split_axis=0, concat_axis=0, tiled=True)  5.38 us
    pallas_call x1, Pallas kernels, local(): pl.pallas_call(prepare_kernel, name='prepare', out_shape=(jax.ShapeDtypeS...  3.36 us
    pallas_call x1, Pallas kernels, local(): pl.pallas_call(functools.partial(contract_kernel, slots=capacity, points=...  3.17 us
  transfers between devices with their start and end apart: 1, of which 1 were waited for; matrix products, arithmetic and copies ran while one was open for 2% of the time, Pallas kernels for 6%

profile of v1, /device:TPU:13, one launch (start us, length us, event | category | flops | bytes accessed | tf_op | source)
XLA Modules:
  0.0 60.9 jit_solution(11870059926976948570)
XLA Ops:
  0.0 0.7 %and_select_fusion.3 = s32[32]{0:T(128)S(1)} fusion(s32[1,32]{1,0:T(1,128)} %param.8), kind=kLoop, calls=%fused_computation.10 | loop fusion | flops 480 | bytes 256 | tf_op jit(solution)/shard_map/jit(floor_divide)/jit(_where)/select_n | solution.py:145
  0.7 0.7 %fusion.2 = (s32[32]{0:T(128)S(1)}, s32[1,32]{1,0:T(1,128)S(1)}) fusion(s32[1,32]{1,0:T(1,128)} %param.8), kind=kLoop, calls=%fused_computation.22 | loop fusion | flops 608 | bytes 384 | tf_op jit(solution)/shard_map/jit(_where)/broadcast_in_dim | solution.py:152
  1.3 0.2 convert_reduce_fusion
  1.5 0.1 select_reduce_fusion
  1.6 0.1 convert_element_type.15
  1.7 0.1 copy.25
  1.8 0.7 %pad.1.clone = f32[8]{0:T(128)S(1)} pad(f32[6]{0:T(128)} %bitcast.47, f32[]{:T(128)} %constant.54), padding=2_0 | pad | bytes 60 | tf_op jit(solution)/shard_map/concatenate | solution.py:154
  2.6 0.1 maximum_bitcast_fusion
  2.6 0.1 copy.26
  2.7 11.1 %all_to_all.17 = f32[16,1,8]{2,1,0:T(1,128)S(1)} all-to-all(f32[16,1,8]{2,1,0:T(1,128)S(1)} %copy.26), channel_id=1, replica_groups=mesh['site'=2,'pts'=16] {'pts'}, dimensions={0} | all-to-all | bytes 1024 | tf_op jit(solution)/shard_map/all_to_all | solution.py:161
  13.8 0.1 copy.27
  13.9 0.1 copy.28
  14.0 0.6 %reshape.67.block_ref = s32[32]{0:T(128)} reshape(s32[16,2]{1,0:T(8,128)S(1)} %copy.28) | data formatting | bytes 256 | tf_op jit(solution)/shard_map/reshape | solution.py:162
  14.6 0.7 %slice.8.mech_ref = f32[16,6]{1,0:T(8,128)} slice(f32[16,8]{1,0:T(8,128)S(1)} %bitcast.43), slice={[0:16], [2:8]} | slice | bytes 768 | tf_op jit(solution)/shard_map/slice | solution.py:163
  15.3 3.2 %contract.1 = f32[32,4,16,128]{3,2,1,0:T(8,128)} custom-call(s32[32]{0:T(128)} %reshape.67.block_ref, f32[16,6]{1,0:T(8,128)} %slice.8.mech_ref, bf16[16,4,6,16,128]{4,3,2,1,0:T(8,128)(2,1)} %bitcast.42), custom_call_target="tpu_custom_call" | custom-call | tf_op jit(solution)/shard_map/contract/pallas_call | solution.py:181
  18.4 0.0 copy-start.1
  18.4 0.0 copy-start.2
  18.4 5.4 %all-to-all-start.1 = ((f32[32,4,16,128]{3,2,1,0:T(8,128)}), f32[32,4,16,128]{3,2,1,0:T(8,128)S(1)}, u32[]{:S(2)}, u32[]{:S(2)}) async-start(f32[32,4,16,128]{3,2,1,0:T(8,128)} %contract.1), calls=%async_computation.1 | async-start | bytes 2097152 | tf_op jit(solution)/shard_map/all_to_all | solution.py:188
  24.5 0.0 copy-done.1
  24.5 0.6 bitcast_select_fusion.weight_ref
  25.1 3.4 %prepare.1 = (bf16[512,1024]{1,0:T(8,128)(2,1)}, bf16[512,1024]{1,0:T(8,128)(2,1)}, bf16[16,256,128]{2,1,0:T(8,128)(2,1)}, bf16[16,256,128]{2,1,0:T(8,128)(2,1)}) custom-call(s32[16,128]{1,0:T(8,128)} %bitcast.44, f32[16,128]{1,0:T(8,128)} %bitcast_select_fusion.weight_ref, f32[16,128]{1,0:T(8,128)} %bitcast.45), custom_call_target="tpu_custom_call" | custom-call | tf_op jit(solution)/shard_map/prepare/pallas_call | solution.py:168
  28.4 0.0 copy-done.2
  28.4 0.6 multiply_add_fusion.row_ref
  29.0 19.7 %all-to-all-done.1.got_ref = f32[32,4,16,128]{3,2,1,0:T(8,128)S(1)} async-done(((f32[32,4,16,128]{3,2,1,0:T(8,128)}), f32[32,4,16,128]{3,2,1,0:T(8,128)S(1)}, u32[]{:S(2)}, u32[]{:S(2)}) %all-to-all-start.1) | async-done | bytes 1048608 | tf_op jit(solution)/shard_map/all_to_all | solution.py:188
  48.8 0.0 copy-start
  48.8 1.0 %copy-done = f32[32,4,16,128]{3,2,1,0:T(8,128)} copy-done((f32[32,4,16,128]{3,2,1,0:T(8,128)}, f32[32,4,16,128]{3,2,1,0:T(8,128)S(1)}, u32[]{:S(2)}) %copy-start) | copy-done | bytes 1048600
  49.7 11.1 %synthesize.1 = f32[16,16,128]{2,1,0:T(8,128)} custom-call(s32[32]{0:T(128)} %multiply_add_fusion.row_ref, f32[32,4,16,128]{3,2,1,0:T(8,128)} %copy-done, bf16[512,1024]{1,0:T(8,128)(2,1)} %get-tuple-element.9.a_hi_ref, bf16[512,1024]{1,0:T(8,128)(2,1)} %get-tuple-element.10.a_lo_ref, bf16[16,256,128]{2,1,0:T(8,128)(2,1)} %get-tuple-element.11.t_hi_ref, ...), custom_call_target="tpu_custom_call" | custom-call | tf_op jit(solution)/shard_map/synthesize/pallas_call | solution.py:190
  (4 shorter events, 0.0 us)
Async XLA Ops:
  18.4 6.0 %copy-start.1 = (f32[1,16,128]{2,1,0:T(8,128)S(1)}, f32[1,16,128]{2,1,0:T(8,128)}, u32[]{:S(2)}) copy-start(f32[1,16,128]{2,1,0:T(8,128)} %param.11) | copy-start | bytes 24580
  18.4 10.0 %copy-start.2 = (s32[1,32]{1,0:T(1,128)S(1)}, s32[1,32]{1,0:T(1,128)}, u32[]{:S(2)}) copy-start(s32[1,32]{1,0:T(1,128)} %param.8) | copy-start | bytes 388
  18.4 30.3 %all-to-all-start.1 = ((f32[32,4,16,128]{3,2,1,0:T(8,128)}), f32[32,4,16,128]{3,2,1,0:T(8,128)S(1)}, u32[]{:S(2)}, u32[]{:S(2)}) async-start(f32[32,4,16,128]{3,2,1,0:T(8,128)} %contract.1), calls=%async_computation.1 | async-start | bytes 2097152 | tf_op jit(solution)/shard_map/all_to_all | solution.py:188
  48.8 1.0 %copy-start = (f32[32,4,16,128]{3,2,1,0:T(8,128)}, f32[32,4,16,128]{3,2,1,0:T(8,128)S(1)}, u32[]{:S(2)}) copy-start(f32[32,4,16,128]{3,2,1,0:T(8,128)S(1)} %all-to-all-done.1.got_ref) | copy-start | bytes 3145732

commit v2 on v1

v2 whole, which is shorter than its diff:
```python
import functools

import jax
import jax.numpy as jnp
from jax import lax
from jax.experimental import pallas as pl
from jax.experimental.pallas import tpu as pltpu
from jax.sharding import PartitionSpec as P

MAXON = 256
FINE = 8
LANES = 128
F32 = jnp.float32
BF16 = jnp.bfloat16


def split(x):
    hi = x.astype(BF16)
    return hi, (x - hi.astype(F32)).astype(BF16)


def dot(a, b):
    return jnp.dot(a, b, preferred_element_type=F32)


def request_kernel(lists_ref, mech_ref, request_ref, slot_ref, *, held, capacity):
    devices = request_ref.shape[0]
    listed = lists_ref.shape[1]
    entries = lists_ref[...].astype(F32)
    holder = jnp.floor((entries + 0.5) * (1.0 / held))
    inside = entries - holder * held
    row = lax.broadcasted_iota(jnp.int32, (listed, listed), 0)
    col = lax.broadcasted_iota(jnp.int32, (listed, listed), 1)
    across = jnp.broadcast_to(holder, (listed, listed))
    down = jnp.sum(jnp.where(row == col, across, 0.0), axis=1, keepdims=True)
    same = jnp.where((down == across) & (row < col), 1.0, 0.0)
    rank = jnp.sum(same, axis=0, keepdims=True)
    slot_ref[...] = (holder * capacity + rank).astype(jnp.int32)
    request_ref[:, capacity:] = jnp.broadcast_to(mech_ref[...], (devices, mech_ref.shape[1]))
    device = lax.broadcasted_iota(jnp.int32, (devices, listed), 0).astype(F32)
    for j in range(capacity):
        hit = (device == holder) & (rank == j)
        request_ref[:, j:j + 1] = jnp.sum(jnp.where(hit, inside, 0.0), axis=1, keepdims=True)


CODE_STEPS = 256.0
CODE_BIAS = 100.0
VALUE_TOP = 32767.0
CODE_ROWS = 8


def encode(x):
    top = jnp.max(jnp.max(jnp.abs(x), axis=0, keepdims=True), axis=1, keepdims=True)
    code = jnp.ceil((jnp.log2(jnp.maximum(top, 1e-30)) + CODE_BIAS) * CODE_STEPS)
    code = jnp.broadcast_to(code, (1, LANES))
    scale = jnp.exp2(15.0 - (code * (1.0 / CODE_STEPS) - CODE_BIAS))
    value = jnp.clip(jnp.floor(x * scale + 0.5), -VALUE_TOP, VALUE_TOP)
    return value.astype(jnp.int32).astype(jnp.int16), code


def decode(y, codes, entry):
    place = lax.broadcasted_iota(jnp.int32, codes.shape, 0)
    code = jnp.sum(jnp.where(place == entry, codes, 0.0), axis=0, keepdims=True)
    scale = jnp.exp2((code * (1.0 / CODE_STEPS) - CODE_BIAS) - 15.0)
    return y.astype(jnp.int32).astype(F32) * scale


def contract_kernel(asked_ref, tensors_ref, out_ref, *, slots, points, strains):
    rows = tensors_ref.shape[3]
    code_rows = out_ref.shape[1] - slots * points * rows

    def one_source(source, carry):
        factors = [asked_ref[source, slots + s] for s in range(strains)]
        place = lax.broadcasted_iota(jnp.int32, (code_rows, LANES), 0)
        codes = jnp.zeros((code_rows, LANES), F32)
        for j in range(slots):
            block = asked_ref[source, j].astype(jnp.int32)
            for p in range(points):
                total = factors[0] * tensors_ref[block, p, 0].astype(F32)
                for s in range(1, strains):
                    total = total + factors[s] * tensors_ref[block, p, s].astype(F32)
                entry = j * points + p
                value, code = encode(total)
                out_ref[source, pl.ds(entry * rows, rows), :] = value
                codes = jnp.where(place == entry, code, codes)
        out_ref[source, pl.ds(slots * points * rows, code_rows), :] = codes.astype(jnp.int32).astype(jnp.int16)
        return carry

    lax.fori_loop(0, out_ref.shape[0], one_source, 0, unroll=2)


def prepare_kernel(onset_ref, weight_ref, rate_ref, a_ref, t_hi_ref, t_lo_ref):
    variations, points = onset_ref.shape
    width = FINE * points
    taps = rate_ref.shape[1]
    onsets = onset_ref[...]
    weights = weight_ref[...]
    w_hi = weights.astype(BF16).astype(F32)
    w_lo = weights - w_hi
    for coarse in range(MAXON // FINE):
        for fine in range(FINE):
            hit = onsets == coarse * FINE + fine
            rows = pl.ds(coarse * variations, variations)
            near = jnp.where(hit, w_hi, 0.0).astype(BF16)
            a_ref[rows, pl.ds(fine * points, points)] = near
            a_ref[rows, pl.ds(width + fine * points, points)] = near
            a_ref[rows, pl.ds(2 * width + fine * points, points)] = jnp.where(hit, w_lo, 0.0).astype(BF16)
    row = lax.broadcasted_iota(jnp.int32, (taps, taps), 0)
    col = lax.broadcasted_iota(jnp.int32, (taps, taps), 1)
    for v in range(variations):
        rates = jnp.broadcast_to(rate_ref[pl.ds(v, 1), :], (taps, taps))
        turned = pltpu.roll(rates, 0, 1, stride=1, stride_axis=0)
        hi, lo = split(jnp.where(col >= row, turned, 0.0))
        t_hi_ref[v, pl.ds(0, taps), :] = hi
        t_lo_ref[v, pl.ds(0, taps), :] = lo
        hi, lo = split(jnp.where(col < row, turned, 0.0))
        t_hi_ref[v, pl.ds(taps, taps), :] = hi
        t_lo_ref[v, pl.ds(taps, taps), :] = lo


def synth_kernel(row_ref, got_ref, a_ref, t_hi_ref, t_lo_ref, out_ref,
                 base_ref, x_ref, acc_ref, motion_ref, *, listed, points, slots):
    variations, rows = out_ref.shape[:2]
    q = listed * points
    comps = 2
    blocks = rows // comps

    code_rows = got_ref.shape[1] - slots * points * rows

    def place(k, carry):
        slot = row_ref[0, k]
        source = slot // slots
        first = (slot % slots) * points
        codes = got_ref[source, pl.ds(slots * points * rows, code_rows), :].astype(jnp.int32).astype(F32)
        for p in range(points):
            value = got_ref[source, pl.ds(pl.multiple_of((first + p) * rows, rows), rows), :]
            base_ref[pl.ds(pl.multiple_of((k * points + p) * rows, rows), rows), :] = decode(value, codes, first + p)
        return carry

    lax.fori_loop(0, listed, place, 0, unroll=4)
    lane = lax.broadcasted_iota(jnp.int32, (q, LANES), 1)
    for c in range(comps):
        before = [jnp.zeros((q, LANES), F32)] * FINE
        for block in range(blocks):
            r = block * comps + c
            here = base_ref[pl.ds(r, q, stride=rows), :]
            at = pl.ds(block * LANES, LANES)
            for fine in range(FINE):
                turned = pltpu.roll(here, fine, 1) if fine else here
                value = jnp.where(lane >= fine, turned, before[fine]) if fine else here
                hi, lo = split(value)
                x_ref[c, pl.ds(fine * q, q), at] = hi
                x_ref[c, pl.ds((FINE + fine) * q, q), at] = lo
                before[fine] = turned
        both = 2 * FINE * q
        acc_ref[c] = dot(a_ref[:, :both], x_ref[c]) + dot(a_ref[:, both:], x_ref[c, :FINE * q])
    lane = lax.broadcasted_iota(jnp.int32, (variations, LANES), 1)
    zero = jnp.zeros((variations, LANES), F32)
    half = LANES // FINE
    far_count = MAXON // LANES
    pad = motion_ref.shape[0] // variations
    motion_ref[...] = jnp.zeros(motion_ref.shape, F32)
    for c in range(comps):
        before = [zero] * half
        for block in range(blocks):
            total = zero
            for coarse in range(half):
                value = zero
                for far in range(far_count):
                    if block - far < 0:
                        continue
                    at = pl.ds((block - far) * LANES, LANES)
                    value = value + acc_ref[c, pl.ds((far * half + coarse) * variations, variations), at]
                turned = pltpu.roll(value, coarse * FINE, 1) if coarse else value
                total = total + (jnp.where(lane >= coarse * FINE, turned, before[coarse]) if coarse else turned)
                before[coarse] = turned
            motion_ref[pl.ds(FINE + block * comps + c, variations, stride=pad), :] = total
    for v in range(variations):
        here = motion_ref[pl.ds(v * pad + FINE, rows), :]
        earlier = motion_ref[pl.ds(v * pad + FINE - comps, rows), :]
        h_hi, h_lo = split(jnp.concatenate([here, earlier], axis=1))
        out_ref[v] = dot(h_hi, t_hi_ref[v]) + (dot(h_lo, t_hi_ref[v]) + dot(h_hi, t_lo_ref[v]))


SMALL = pltpu.CompilerParams(vmem_limit_bytes=8 << 20)
LARGE = pltpu.CompilerParams(vmem_limit_bytes=20 << 20)
VMEM = pl.BlockSpec(memory_space=pltpu.VMEM)
SMEM = pl.BlockSpec(memory_space=pltpu.SMEM)


def local(green_tensors, block_lists, block_count, onset_steps, slip_amount, mechanism, slip_rate):
    held, points, strains, comps, length = green_tensors.shape
    ruptures, listed = block_lists.shape
    variations = onset_steps.shape[1]
    taps = slip_rate.shape[-1]
    devices = lax.axis_size("pts")
    capacity = max(1, ruptures * listed // devices)
    blocks = length // LANES
    rows = blocks * comps
    q = listed * points

    tensors = green_tensors.reshape(held, points, strains, comps, blocks, LANES)
    tensors = tensors.transpose(0, 1, 2, 4, 3, 5).reshape(held, points, strains, rows, LANES)

    request, slot_of = pl.pallas_call(
        functools.partial(request_kernel, held=held, capacity=capacity),
        name="request",
        out_shape=(
            jax.ShapeDtypeStruct((devices, capacity + strains), F32),
            jax.ShapeDtypeStruct((ruptures, listed), jnp.int32),
        ),
        compiler_params=SMALL,
    )(block_lists, mechanism)
    asked = lax.all_to_all(request, "pts", split_axis=0, concat_axis=0, tiled=True)

    kept = (jnp.arange(q, dtype=jnp.int32) // points) < block_count[0]
    weights = jnp.where(kept[None, :], slip_amount[0], 0.0)
    coarse_rows = MAXON // FINE * variations
    prepared = pl.pallas_call(
        prepare_kernel,
        name="prepare",
        out_shape=(
            jax.ShapeDtypeStruct((coarse_rows, 3 * FINE * q), BF16),
            jax.ShapeDtypeStruct((variations, 2 * taps, taps), BF16),
            jax.ShapeDtypeStruct((variations, 2 * taps, taps), BF16),
        ),
        in_specs=[VMEM, VMEM, VMEM],
        out_specs=(VMEM, VMEM, VMEM),
        compiler_params=SMALL,
    )(onset_steps[0], weights, slip_rate[0])

    code_rows = -(-capacity * points // CODE_ROWS) * CODE_ROWS
    outgoing = pl.pallas_call(
        functools.partial(contract_kernel, slots=capacity, points=points, strains=strains),
        name="contract",
        out_shape=jax.ShapeDtypeStruct((devices, capacity * points * rows + code_rows, LANES), jnp.int16),
        in_specs=[SMEM, VMEM],
        out_specs=VMEM,
        compiler_params=SMALL,
    )(asked, tensors)
    incoming = lax.all_to_all(outgoing, "pts", split_axis=0, concat_axis=0, tiled=True)

    result = pl.pallas_call(
        functools.partial(synth_kernel, listed=listed, points=points, slots=capacity),
        name="synthesize",
        out_shape=jax.ShapeDtypeStruct((variations, rows, LANES), F32),
        in_specs=[SMEM, VMEM, VMEM, VMEM, VMEM],
        out_specs=VMEM,
        compiler_params=LARGE,
        scratch_shapes=[
            pltpu.VMEM((q * rows, LANES), F32),
            pltpu.VMEM((comps, 2 * FINE * q, blocks * LANES), BF16),
            pltpu.VMEM((comps, coarse_rows, blocks * LANES), F32),
            pltpu.VMEM((variations * (rows + FINE), LANES), F32),
        ],
    )(slot_of, incoming, *prepared)
    result = result.reshape(variations, blocks, comps, LANES).transpose(0, 2, 1, 3)
    return result.reshape(1, variations, comps, length)


def solution(mesh):
    in_specs = (
        P(("site", "pts"), None, None, None, None),
        P(("site", "pts"), None),
        P(("site", "pts")),
        P(("site", "pts"), None, None),
        P(("site", "pts"), None, None),
        P(("site", "pts"), None),
        P(("site", "pts"), None, None),
    )
    out_specs = P(("site", "pts"), None, None, None)
    return jax.shard_map(local, mesh=mesh, in_specs=in_specs, out_specs=out_specs, check_vma=False)
```

time: 61.2 us -> 51.9 us (0.85)
  the two profiles are of different devices: /device:TPU:13 before, /device:TPU:0 now
where the time goes in v2:
time: 51.9 us; the launch traced here: 51.4 us
  Pallas kernels  14.2 us (27%)
  blocking collectives  13.6 us (26%)
  waiting for transfers between devices  11.4 us (22%)
  local copies, waits for them, and re-layouts  7.16 us (14%)
  starting transfers between devices  4.25 us (8%)
  between operations  0.72 us (1%)
    all_to_all x1, blocking collectives, local(): lax.all_to_all(request, 'pts', split_axis=0, concat_axis=0, tiled=True)  13.6 us
    all_to_all x1, waiting for transfers between devices, local(): lax.all_to_all(outgoing, 'pts', split_axis=0, concat_axis=0, tiled=True)  11.4 us
    pallas_call x1, Pallas kernels, local(): pl.pallas_call(functools.partial(synth_kernel, listed=listed, points=poin...  10.1 us
    unnamed x20, local copies, waits for them, and re-layouts  7.16 us
    all_to_all x1, starting transfers between devices, local(): lax.all_to_all(outgoing, 'pts', split_axis=0, concat_axis=0, tiled=True)  4.25 us
    pallas_call x1, Pallas kernels, local(): pl.pallas_call(functools.partial(contract_kernel, slots=capacity, points=...  3.17 us
  transfers between devices with their start and end apart: 1, of which 1 were waited for; matrix products, arithmetic and copies ran while one was open for 0% of the time, Pallas kernels for 2%

profile of v2, /device:TPU:0, one launch (start us, length us, event | category | flops | bytes accessed | tf_op | source)
XLA Modules:
  0.0 51.4 jit_solution(11718930531834862616)
XLA Ops:
  0.0 0.0 copy-start.6
  0.0 0.0 copy-start.7
  0.0 0.7 %copy-done.7 = s32[1,32]{1,0:T(1,128)S(1)} copy-done((s32[1,32]{1,0:T(1,128)S(1)}, s32[1,32]{1,0:T(1,128)}, u32[]{:S(2)}) %copy-start.7) | copy-done | bytes 152
  0.7 0.0 copy-start.8
  0.7 0.7 %copy-done.8 = f32[1,6]{1,0:T(1,128)S(1)} copy-done((f32[1,6]{1,0:T(1,128)S(1)}, f32[1,6]{1,0:T(1,128)}, u32[]{:S(2)}) %copy-start.8) | copy-done | bytes 48
  1.3 0.0 copy-start.9
  1.3 0.0 copy-start.5
  1.3 0.2 request.1
  1.5 13.6 %all_to_all.16 = f32[16,1,8]{2,1,0:T(1,128)S(1)} all-to-all(f32[16,1,8]{2,1,0:T(1,128)S(1)} %bitcast.24), channel_id=1, replica_groups=mesh['site'=2,'pts'=16] {'pts'}, dimensions={0} | all-to-all | bytes 1024 | tf_op jit(solution)/shard_map/all_to_all | solution.py:214
  15.1 0.0 copy-start
  15.1 1.4 %copy-done = bf16[16,4,6,2,1024]{4,3,2,1,0:T(2,128)(2,1)S(1)} copy-done((bf16[16,4,6,2,1024]{4,3,2,1,0:T(2,128)(2,1)S(1)}, bf16[16,4,6,2,1024]{4,3,2,1,0:T(2,128)(2,1)}, u32[]{:S(2)}) %copy-start) | copy-done | bytes 1572888
  16.5 3.2 %contract.1 = s16[16,136,128]{2,1,0:T(8,128)(2,1)} custom-call(f32[16,8]{1,0:T(8,128)S(1)} %bitcast.21, bf16[16,4,6,16,128]{4,3,2,1,0:T(8,128)(2,1)S(1)} %bitcast.20), custom_call_target="tpu_custom_call" | custom-call | tf_op jit(solution)/shard_map/contract/pallas_call | solution.py:233
  19.7 4.3 %all-to-all-start.1 = ((s16[16,136,128]{2,1,0:T(8,128)(2,1)}), s16[16,136,128]{2,1,0:T(8,128)(2,1)}, u32[]{:S(2)}, u32[]{:S(2)}) async-start(s16[16,136,128]{2,1,0:T(8,128)(2,1)} %contract.1), calls=%async_computation.1 | async-start | bytes 1114112 | tf_op jit(solution)/shard_map/all_to_all | solution.py:241
  24.6 0.0 copy-done.9
  24.6 0.0 copy-done.6
  24.7 0.0 copy-done.5
  24.7 0.8 %prepare.1 = (bf16[512,3072]{1,0:T(8,128)(2,1)S(1)}, bf16[16,256,128]{2,1,0:T(8,128)(2,1)S(1)}, bf16[16,256,128]{2,1,0:T(8,128)(2,1)S(1)}) custom-call(s32[16,128]{1,0:T(8,128)S(1)} %bitcast.22, f32[16,128]{1,0:T(8,128)S(1)} %bitcast_select_fusion.weight_ref, f32[16,128]{1,0:T(8,128)S(1)} %bitcast.23), custom_call_target="tpu_custom_call" | custom-call | tf_op jit(solution)/shard_map/prepare/pallas_call | solution.py:219
  25.5 0.0 copy-start.1
  25.5 1.0 %copy-done.1 = bf16[16,256,128]{2,1,0:T(8,128)(2,1)} copy-done((bf16[16,256,128]{2,1,0:T(8,128)(2,1)}, bf16[16,256,128]{2,1,0:T(8,128)(2,1)S(1)}, u32[]{:S(2)}) %copy-start.1) | copy-done | bytes 1048600
  26.4 0.0 copy-start.3
  26.4 1.0 %copy-done.3 = bf16[16,256,128]{2,1,0:T(8,128)(2,1)} copy-done((bf16[16,256,128]{2,1,0:T(8,128)(2,1)}, bf16[16,256,128]{2,1,0:T(8,128)(2,1)S(1)}, u32[]{:S(2)}) %copy-start.3) | copy-done | bytes 1048600
  27.4 11.4 %all-to-all-done.1.got_ref = s16[16,136,128]{2,1,0:T(8,128)(2,1)} async-done(((s16[16,136,128]{2,1,0:T(8,128)(2,1)}), s16[16,136,128]{2,1,0:T(8,128)(2,1)}, u32[]{:S(2)}, u32[]{:S(2)}) %all-to-all-start.1) | async-done | bytes 557088 | tf_op jit(solution)/shard_map/all_to_all | solution.py:241
  38.8 0.0 copy-start.2
  38.8 1.2 %copy-done.2 = bf16[16,256,128]{2,1,0:T(8,128)(2,1)S(1)} copy-done((bf16[16,256,128]{2,1,0:T(8,128)(2,1)S(1)}, bf16[16,256,128]{2,1,0:T(8,128)(2,1)}, u32[]{:S(2)}) %copy-start.2) | copy-done | bytes 1048600
  40.0 0.0 copy-start.4
  40.0 1.2 %copy-done.4 = bf16[16,256,128]{2,1,0:T(8,128)(2,1)S(1)} copy-done((bf16[16,256,128]{2,1,0:T(8,128)(2,1)S(1)}, bf16[16,256,128]{2,1,0:T(8,128)(2,1)}, u32[]{:S(2)}) %copy-start.4) | copy-done | bytes 1048600
  41.2 10.1 %synthesize.1 = f32[16,16,128]{2,1,0:T(8,128)} custom-call(s32[1,32]{1,0:T(1,128)S(1)} %get-tuple-element.10.row_ref, s16[16,136,128]{2,1,0:T(8,128)(2,1)} %all-to-all-done.1.got_ref, bf16[512,3072]{1,0:T(8,128)(2,1)S(1)} %get-tuple-element.12.a_ref, bf16[16,256,128]{2,1,0:T(8,128)(2,1)S(1)} %copy-done.2, bf16[16,256,128]{2,1,0:T(8,128)(2,1)S(1)} %copy-done.4), custom_call_target="tpu_custom_call" | custom-call | tf_op jit(solution)/shard_map/synthesize/pallas_call | solution.py:243
  (2 shorter events, 0.0 us)
Async XLA Ops:
  0.0 24.6 %copy-start.6 = (f32[1,16,128]{2,1,0:T(8,128)S(1)}, f32[1,16,128]{2,1,0:T(8,128)}, u32[]{:S(2)}) copy-start(f32[1,16,128]{2,1,0:T(8,128)} %param.13) | copy-start | bytes 24580
  0.0 0.7 %copy-start.7 = (s32[1,32]{1,0:T(1,128)S(1)}, s32[1,32]{1,0:T(1,128)}, u32[]{:S(2)}) copy-start(s32[1,32]{1,0:T(1,128)} %lists_ref.1) | copy-start | bytes 388
  0.7 0.7 %copy-start.8 = (f32[1,6]{1,0:T(1,128)S(1)}, f32[1,6]{1,0:T(1,128)}, u32[]{:S(2)}) copy-start(f32[1,6]{1,0:T(1,128)} %mech_ref.1) | copy-start | bytes 76
  1.3 23.3 %copy-start.9 = (f32[1,16,128]{2,1,0:T(8,128)S(1)}, f32[1,16,128]{2,1,0:T(8,128)}, u32[]{:S(2)}) copy-start(f32[1,16,128]{2,1,0:T(8,128)} %param.11) | copy-start | bytes 24580
  1.3 23.3 %copy-start.5 = (s32[1,16,128]{2,1,0:T(8,128)S(1)}, s32[1,16,128]{2,1,0:T(8,128)}, u32[]{:S(2)}) copy-start(s32[1,16,128]{2,1,0:T(8,128)} %param.10) | copy-start | bytes 24580
  15.1 1.4 %copy-start = (bf16[16,4,6,2,1024]{4,3,2,1,0:T(2,128)(2,1)S(1)}, bf16[16,4,6,2,1024]{4,3,2,1,0:T(2,128)(2,1)}, u32[]{:S(2)}) copy-start(bf16[16,4,6,2,1024]{4,3,2,1,0:T(2,128)(2,1)} %param.7) | copy-start | bytes 4718596
  19.7 19.1 %all-to-all-start.1 = ((s16[16,136,128]{2,1,0:T(8,128)(2,1)}), s16[16,136,128]{2,1,0:T(8,128)(2,1)}, u32[]{:S(2)}, u32[]{:S(2)}) async-start(s16[16,136,128]{2,1,0:T(8,128)(2,1)} %contract.1), calls=%async_computation.1 | async-start | bytes 1114112 | tf_op jit(solution)/shard_map/all_to_all | solution.py:241
  25.5 1.0 %copy-start.1 = (bf16[16,256,128]{2,1,0:T(8,128)(2,1)}, bf16[16,256,128]{2,1,0:T(8,128)(2,1)S(1)}, u32[]{:S(2)}) copy-start(bf16[16,256,128]{2,1,0:T(8,128)(2,1)S(1)} %get-tuple-element.13.t_hi_ref) | copy-start | bytes 3145732
  26.4 1.0 %copy-start.3 = (bf16[16,256,128]{2,1,0:T(8,128)(2,1)}, bf16[16,256,128]{2,1,0:T(8,128)(2,1)S(1)}, u32[]{:S(2)}) copy-start(bf16[16,256,128]{2,1,0:T(8,128)(2,1)S(1)} %get-tuple-element.14.t_lo_ref) | copy-start | bytes 3145732
  38.8 1.2 %copy-start.2 = (bf16[16,256,128]{2,1,0:T(8,128)(2,1)S(1)}, bf16[16,256,128]{2,1,0:T(8,128)(2,1)}, u32[]{:S(2)}) copy-start(bf16[16,256,128]{2,1,0:T(8,128)(2,1)} %copy-done.1) | copy-start | bytes 3145732
  40.0 1.2 %copy-start.4 = (bf16[16,256,128]{2,1,0:T(8,128)(2,1)S(1)}, bf16[16,256,128]{2,1,0:T(8,128)(2,1)}, u32[]{:S(2)}) copy-start(bf16[16,256,128]{2,1,0:T(8,128)(2,1)} %copy-done.3) | copy-start | bytes 3145732

commit v3 on v2

--- a/solution.py
+++ b/solution.py
@@ -89,10 +89,9 @@
     lax.fori_loop(0, out_ref.shape[0], one_source, 0, unroll=2)
 
 
-def prepare_kernel(onset_ref, weight_ref, rate_ref, a_ref, t_hi_ref, t_lo_ref):
+def prepare_kernel(onset_ref, weight_ref, a_ref):
     variations, points = onset_ref.shape
     width = FINE * points
-    taps = rate_ref.shape[1]
     onsets = onset_ref[...]
     weights = weight_ref[...]
     w_hi = weights.astype(BF16).astype(F32)
@@ -105,20 +104,9 @@
             a_ref[rows, pl.ds(fine * points, points)] = near
             a_ref[rows, pl.ds(width + fine * points, points)] = near
             a_ref[rows, pl.ds(2 * width + fine * points, points)] = jnp.where(hit, w_lo, 0.0).astype(BF16)
-    row = lax.broadcasted_iota(jnp.int32, (taps, taps), 0)
-    col = lax.broadcasted_iota(jnp.int32, (taps, taps), 1)
-    for v in range(variations):
-        rates = jnp.broadcast_to(rate_ref[pl.ds(v, 1), :], (taps, taps))
-        turned = pltpu.roll(rates, 0, 1, stride=1, stride_axis=0)
-        hi, lo = split(jnp.where(col >= row, turned, 0.0))
-        t_hi_ref[v, pl.ds(0, taps), :] = hi
-        t_lo_ref[v, pl.ds(0, taps), :] = lo
-        hi, lo = split(jnp.where(col < row, turned, 0.0))
-        t_hi_ref[v, pl.ds(taps, taps), :] = hi
-        t_lo_ref[v, pl.ds(taps, taps), :] = lo
-
-
-def synth_kernel(row_ref, got_ref, a_ref, t_hi_ref, t_lo_ref, out_ref,
+
+
+def synth_kernel(row_ref, got_ref, a_ref, rate_ref, out_ref,
                  base_ref, x_ref, acc_ref, motion_ref, *, listed, points, slots):
     variations, rows = out_ref.shape[:2]
     q = listed * points
@@ -175,11 +163,18 @@
                 total = total + (jnp.where(lane >= coarse * FINE, turned, before[coarse]) if coarse else turned)
                 before[coarse] = turned
             motion_ref[pl.ds(FINE + block * comps + c, variations, stride=pad), :] = total
+    taps = rate_ref.shape[1]
+    row = lax.broadcasted_iota(jnp.int32, (taps, taps), 0)
+    col = lax.broadcasted_iota(jnp.int32, (taps, taps), 1)
     for v in range(variations):
+        rates = jnp.broadcast_to(rate_ref[pl.ds(v, 1), :], (taps, taps))
+        turned = pltpu.roll(rates, 0, 1, stride=1, stride_axis=0)
+        spread = [jnp.where(col >= row, turned, 0.0), jnp.where(col < row, turned, 0.0)]
+        t_hi, t_lo = split(jnp.concatenate(spread, axis=0))
         here = motion_ref[pl.ds(v * pad + FINE, rows), :]
         earlier = motion_ref[pl.ds(v * pad + FINE - comps, rows), :]
         h_hi, h_lo = split(jnp.concatenate([here, earlier], axis=1))
-        out_ref[v] = dot(h_hi, t_hi_ref[v]) + (dot(h_lo, t_hi_ref[v]) + dot(h_hi, t_lo_ref[v]))
+        out_ref[v] = dot(h_hi, t_hi) + (dot(h_lo, t_hi) + dot(h_hi, t_lo))
 
 
 SMALL = pltpu.CompilerParams(vmem_limit_bytes=8 << 20)
@@ -192,7 +187,6 @@
     held, points, strains, comps, length = green_tensors.shape
     ruptures, listed = block_lists.shape
     variations = onset_steps.shape[1]
-    taps = slip_rate.shape[-1]
     devices = lax.axis_size("pts")
     capacity = max(1, ruptures * listed // devices)
     blocks = length // LANES
@@ -219,15 +213,11 @@
     prepared = pl.pallas_call(
         prepare_kernel,
         name="prepare",
-        out_shape=(
-            jax.ShapeDtypeStruct((coarse_rows, 3 * FINE * q), BF16),
-            jax.ShapeDtypeStruct((variations, 2 * taps, taps), BF16),
-            jax.ShapeDtypeStruct((variations, 2 * taps, taps), BF16),
-        ),
-        in_specs=[VMEM, VMEM, VMEM],
-        out_specs=(VMEM, VMEM, VMEM),
+        out_shape=jax.ShapeDtypeStruct((coarse_rows, 3 * FINE * q), BF16),
+        in_specs=[VMEM, VMEM],
+        out_specs=VMEM,
         compiler_params=SMALL,
-    )(onset_steps[0], weights, slip_rate[0])
+    )(onset_steps[0], weights)
 
     code_rows = -(-capacity * points // CODE_ROWS) * CODE_ROWS
     outgoing = pl.pallas_call(
@@ -244,7 +234,7 @@
         functools.partial(synth_kernel, listed=listed, points=points, slots=capacity),
         name="synthesize",
         out_shape=jax.ShapeDtypeStruct((variations, rows, LANES), F32),
-        in_specs=[SMEM, VMEM, VMEM, VMEM, VMEM],
+        in_specs=[SMEM, VMEM, VMEM, VMEM],
         out_specs=VMEM,
         compiler_params=LARGE,
         scratch_shapes=[
@@ -253,7 +243,7 @@
             pltpu.VMEM((comps, coarse_rows, blocks * LANES), F32),
             pltpu.VMEM((variations * (rows + FINE), LANES), F32),
         ],
-    )(slot_of, incoming, *prepared)
+    )(slot_of, incoming, prepared, slip_rate[0])
     result = result.reshape(variations, blocks, comps, LANES).transpose(0, 2, 1, 3)
     return result.reshape(1, variations, comps, length)
 

time: 51.9 us -> 49.4 us (0.952)
  local copies, waits for them, and re-layouts: 7.16 us -> 2.74 us
  waiting for transfers between devices: 11.4 us -> 13.7 us
    unnamed x20 -> x12, local copies, waits for them, and re-layouts: 7.16 us -> 2.74 us
    all_to_all x1, waiting for transfers between devices: 11.4 us -> 13.7 us  [local(): lax.all_to_all(outgoing, 'pts', split_axis=0, concat_axis=0, tiled=True)]
  transfers between devices with their start and end apart: 1 -> 1, of which waited for: 1 -> 1; matrix products, arithmetic and copies ran while one was open for 0% -> 0% of each run, Pallas kernels for 2% -> 1%
where the time goes in v3:
time: 49.4 us; the launch traced here: 49 us
  Pallas kernels  13.9 us (28%)
  waiting for transfers between devices  13.7 us (28%)
  blocking collectives  13.6 us (28%)
  starting transfers between devices  4.24 us (9%)
  local copies, waits for them, and re-layouts  2.74 us (6%)
  between operations  0.7 us (1%)
    all_to_all x1, waiting for transfers between devices, local(): lax.all_to_all(outgoing, 'pts', split_axis=0, concat_axis=0, tiled=True)  13.7 us
    all_to_all x1, blocking collectives, local(): lax.all_to_all(request, 'pts', split_axis=0, concat_axis=0, tiled=True)  13.6 us
    pallas_call x1, Pallas kernels, local(): pl.pallas_call(functools.partial(synth_kernel, listed=listed, points=poin...  10.2 us
    all_to_all x1, starting transfers between devices, local(): lax.all_to_all(outgoing, 'pts', split_axis=0, concat_axis=0, tiled=True)  4.24 us
    pallas_call x1, Pallas kernels, local(): pl.pallas_call(functools.partial(contract_kernel, slots=capacity, points=...  3.17 us
    unnamed x12, local copies, waits for them, and re-layouts  2.74 us
  transfers between devices with their start and end apart: 1, of which 1 were waited for; matrix products, arithmetic and copies ran while one was open for 0% of the time, Pallas kernels for 1%

profile of v3, /device:TPU:0, one launch (start us, length us, event | category | flops | bytes accessed | tf_op | source)
XLA Modules:
  0.0 49.0 jit_solution(13305952488654087654)
XLA Ops:
  0.0 0.0 copy-start.1
  0.0 0.0 copy-start.3
  0.0 0.7 %copy-done.3 = s32[1,32]{1,0:T(1,128)S(1)} copy-done((s32[1,32]{1,0:T(1,128)S(1)}, s32[1,32]{1,0:T(1,128)}, u32[]{:S(2)}) %copy-start.3) | copy-done | bytes 152
  0.7 0.0 copy-start.4
  0.7 0.7 %copy-done.4 = f32[1,6]{1,0:T(1,128)S(1)} copy-done((f32[1,6]{1,0:T(1,128)S(1)}, f32[1,6]{1,0:T(1,128)}, u32[]{:S(2)}) %copy-start.4) | copy-done | bytes 48
  1.3 0.0 copy-start.5
  1.3 0.2 request.1
  1.5 13.6 %all_to_all.16 = f32[16,1,8]{2,1,0:T(1,128)S(1)} all-to-all(f32[16,1,8]{2,1,0:T(1,128)S(1)} %bitcast.24), channel_id=1, replica_groups=mesh['site'=2,'pts'=16] {'pts'}, dimensions={0} | all-to-all | bytes 1024 | tf_op jit(solution)/shard_map/all_to_all | solution.py:208
  15.1 0.0 copy-start
  15.1 1.4 %copy-done = bf16[16,4,6,2,1024]{4,3,2,1,0:T(2,128)(2,1)S(1)} copy-done((bf16[16,4,6,2,1024]{4,3,2,1,0:T(2,128)(2,1)S(1)}, bf16[16,4,6,2,1024]{4,3,2,1,0:T(2,128)(2,1)}, u32[]{:S(2)}) %copy-start) | copy-done | bytes 1572888
  16.5 0.0 copy-start.2
  16.5 3.2 %contract.1 = s16[16,136,128]{2,1,0:T(8,128)(2,1)} custom-call(f32[16,8]{1,0:T(8,128)S(1)} %bitcast.21, bf16[16,4,6,16,128]{4,3,2,1,0:T(8,128)(2,1)S(1)} %bitcast.20), custom_call_target="tpu_custom_call" | custom-call | tf_op jit(solution)/shard_map/contract/pallas_call | solution.py:223
  19.7 4.2 %all-to-all-start.1 = ((s16[16,136,128]{2,1,0:T(8,128)(2,1)}), s16[16,136,128]{2,1,0:T(8,128)(2,1)}, u32[]{:S(2)}, u32[]{:S(2)}) async-start(s16[16,136,128]{2,1,0:T(8,128)(2,1)} %contract.1), calls=%async_computation.1 | async-start | bytes 1114112 | tf_op jit(solution)/shard_map/all_to_all | solution.py:231
  24.6 0.0 copy-done.5
  24.6 0.0 copy-done.1
  24.6 0.4 prepare.1.a_ref
  25.1 13.7 %all-to-all-done.1.got_ref = s16[16,136,128]{2,1,0:T(8,128)(2,1)} async-done(((s16[16,136,128]{2,1,0:T(8,128)(2,1)}), s16[16,136,128]{2,1,0:T(8,128)(2,1)}, u32[]{:S(2)}, u32[]{:S(2)}) %all-to-all-start.1) | async-done | bytes 557088 | tf_op jit(solution)/shard_map/all_to_all | solution.py:231
  38.8 0.0 copy-done.2
  38.8 10.2 %synthesize.1 = f32[16,16,128]{2,1,0:T(8,128)} custom-call(s32[1,32]{1,0:T(1,128)S(1)} %get-tuple-element.7.row_ref, s16[16,136,128]{2,1,0:T(8,128)(2,1)} %all-to-all-done.1.got_ref, bf16[512,3072]{1,0:T(8,128)(2,1)S(1)} %prepare.1.a_ref, f32[16,128]{1,0:T(8,128)S(1)} %bitcast.23), custom_call_target="tpu_custom_call" | custom-call | tf_op jit(solution)/shard_map/synthesize/pallas_call | solution.py:233
  (2 shorter events, 0.0 us)
Async XLA Ops:
  0.0 24.6 %copy-start.1 = (s32[1,16,128]{2,1,0:T(8,128)S(1)}, s32[1,16,128]{2,1,0:T(8,128)}, u32[]{:S(2)}) copy-start(s32[1,16,128]{2,1,0:T(8,128)} %param.10) | copy-start | bytes 24580
  0.0 0.7 %copy-start.3 = (s32[1,32]{1,0:T(1,128)S(1)}, s32[1,32]{1,0:T(1,128)}, u32[]{:S(2)}) copy-start(s32[1,32]{1,0:T(1,128)} %lists_ref.1) | copy-start | bytes 388
  0.7 0.7 %copy-start.4 = (f32[1,6]{1,0:T(1,128)S(1)}, f32[1,6]{1,0:T(1,128)}, u32[]{:S(2)}) copy-start(f32[1,6]{1,0:T(1,128)} %mech_ref.1) | copy-start | bytes 76
  1.3 23.3 %copy-start.5 = (f32[1,16,128]{2,1,0:T(8,128)S(1)}, f32[1,16,128]{2,1,0:T(8,128)}, u32[]{:S(2)}) copy-start(f32[1,16,128]{2,1,0:T(8,128)} %param.11) | copy-start | bytes 24580
  15.1 1.4 %copy-start = (bf16[16,4,6,2,1024]{4,3,2,1,0:T(2,128)(2,1)S(1)}, bf16[16,4,6,2,1024]{4,3,2,1,0:T(2,128)(2,1)}, u32[]{:S(2)}) copy-start(bf16[16,4,6,2,1024]{4,3,2,1,0:T(2,128)(2,1)} %param.7) | copy-start | bytes 4718596
  16.5 22.2 %copy-start.2 = (f32[1,16,128]{2,1,0:T(8,128)S(1)}, f32[1,16,128]{2,1,0:T(8,128)}, u32[]{:S(2)}) copy-start(f32[1,16,128]{2,1,0:T(8,128)} %param.13) | copy-start | bytes 24580
  19.7 19.1 %all-to-all-start.1 = ((s16[16,136,128]{2,1,0:T(8,128)(2,1)}), s16[16,136,128]{2,1,0:T(8,128)(2,1)}, u32[]{:S(2)}, u32[]{:S(2)}) async-start(s16[16,136,128]{2,1,0:T(8,128)(2,1)} %contract.1), calls=%async_computation.1 | async-start | bytes 1114112 | tf_op jit(solution)/shard_map/all_to_all | solution.py:231
